TPU v7x, 128 devices: a whole 4x4x4 slice. The times are simulated.
128 devices in a mesh: row: 16 (over z_hi, x, core), col: 8 (over y, z_lo).
Axes of the slice: x: 4, y: 4, z: 4 (z_hi: 2, z_lo: 2; z = z_hi * 2 + z_lo), core: 2. Of those that a mesh axis runs over, the one named last changes fastest.
Arguments:
- pair: bfloat16 [512, 512, 128], P('row', 'col'), may hold values from -6 to 6
- cotangent: bfloat16 [512, 512, 128], P('row', 'col'), may hold values from -6 to 6
- length: int32 [1], replicated, may hold values from 256 to 512
- norm_gain: float32 [128], replicated, may hold values from 0.1 to 1.9
- norm_bias: float32 [128], replicated, may hold values from -1.5 to 1.5
- left_weight: bfloat16 [128, 256], replicated, may hold values from -0.5 to 0.5
- right_weight: bfloat16 [128, 256], replicated, may hold values from -0.5 to 0.5
- gate_weight: bfloat16 [128, 128], replicated, may hold values from -0.5 to 0.5
- out_gain: float32 [128], replicated, may hold values from 0.1 to 1.9
- out_bias: float32 [128], replicated, may hold values from -2 to 2
- out_weight: bfloat16 [128, 128], replicated, may hold values from -0.5 to 0.5
Outputs:
- update: bfloat16 [512, 512, 128], P('row', 'col')
- grad_pair: bfloat16 [512, 512, 128], P('row', 'col')
- grad_left: float32 [128, 256], replicated
- grad_right: float32 [128, 256], replicated
- grad_gating: float32 [128, 128], replicated
- grad_output: float32 [128, 128], replicated
- grad_norms: float32 [4, 128], replicated
Inputs may be any that keep to these rules, and one draw needn't show every extreme that they name: Tokens at positions 511 down to length are padding.
All inputs are finite; a program needn't handle non-finite values.
Results may differ from a plain program's by a relative error of at most 0.014.
Values may be sent and summed in bfloat16 or wider, within the bound.
A program may use at most 128 MiB of HBM per device.

v0:
```python
import jax
import jax.numpy as jnp
from jax import lax
from jax.sharding import PartitionSpec as P

EPS = 1e-05
AXES = ("row", "col")


def normalize(values):
    center = values - jnp.mean(values, axis=-1, keepdims=True)
    inverse = lax.rsqrt(jnp.mean(center * center, axis=-1, keepdims=True) + EPS)
    return (center * inverse, inverse)


def exchange(x):
    return lax.all_to_all(x, AXES, 0, 0, tiled=True)


def per_device(
    pair,
    cotangent,
    length,
    norm_gain,
    norm_bias,
    left_weight,
    right_weight,
    gate_weight,
    out_gain,
    out_bias,
    out_weight,
):
    n_row = lax.axis_size("row")
    n_col = lax.axis_size("col")
    n = n_row * n_col
    rows, cols = pair.shape[:2]
    tokens = rows * n_row
    hidden = out_weight.shape[0]
    row_at = lax.axis_index("row") * rows
    col_at = lax.axis_index("col") * cols
    first_ok = row_at + jnp.arange(rows, dtype=jnp.int32) < length[0]
    second_ok = col_at + jnp.arange(cols, dtype=jnp.int32) < length[0]
    mask = (first_ok[:, None] & second_ok[None, :]).astype(jnp.float32).reshape(1, -1)

    def to_owner(tiles):
        return exchange(jnp.stack([t.reshape(n, rows * cols // 128, 128) for t in tiles], axis=1))

    def whole(received):
        return (
            received.reshape(n_row, n_col, rows, cols).transpose(0, 2, 1, 3).reshape(tokens, tokens)
        )

    def tiled(matrix):
        t = matrix.reshape(n_row, rows, n_col, cols).transpose(0, 2, 1, 3)
        return t.reshape(n, rows * cols // 128, 128)

    pair_hat, pair_scale = normalize(pair.astype(jnp.float32))
    normed = (pair_hat * norm_gain + norm_bias).astype(jnp.bfloat16)
    flat = normed.reshape(rows * cols, -1)

    def dot(form, a, b):
        return jnp.einsum(form, a, b, preferred_element_type=jnp.float32)

    def gating(weight):
        projected = dot("pc,ch->hp", flat, weight)
        values = projected[:hidden]
        sig = jax.nn.sigmoid(projected[hidden:])
        return ((mask * sig * values).astype(jnp.bfloat16), values, sig)

    left, left_val, left_sig = gating(left_weight)
    right, right_val, right_sig = gating(right_weight)
    got = to_owner([left, right])
    big_l = whole(got[:, 0])
    big_r = whole(got[:, 1])
    tri_own = dot("ik,jk->ij", big_l, big_r).astype(jnp.bfloat16)
    tri = exchange(tiled(tri_own)).reshape(hidden, -1).astype(jnp.float32)
    center = tri - jnp.mean(tri, axis=0, keepdims=True)
    tri_scale = lax.rsqrt(jnp.mean(center * center, axis=0, keepdims=True) + EPS)
    tri_hat = center * tri_scale
    tri_normed = (tri_hat * out_gain[:, None] + out_bias[:, None]).astype(jnp.bfloat16)
    outer = dot("hp,hc->cp", tri_normed, out_weight)
    gate = jax.nn.sigmoid(dot("pc,cd->dp", flat, gate_weight))
    update = (gate * outer).astype(jnp.bfloat16).T.reshape(pair.shape)
    upstream = cotangent.reshape(rows * cols, -1).T.astype(jnp.float32)
    outer_grad = (upstream * gate).astype(jnp.bfloat16)
    gate_grad = (upstream * outer * gate * (1.0 - gate)).astype(jnp.bfloat16)
    grad_output = dot("hp,cp->hc", tri_normed, outer_grad)
    grad_gating = dot("pc,dp->cd", flat, gate_grad)
    tnorm_grad = dot("cp,hc->hp", outer_grad, out_weight)
    hat_grad = tnorm_grad * out_gain[:, None]
    tri_grad = (
        tri_scale
        * (
            hat_grad
            - jnp.mean(hat_grad, axis=0, keepdims=True)
            - tri_hat * jnp.mean(hat_grad * tri_hat, axis=0, keepdims=True)
        )
    ).astype(jnp.bfloat16)
    g = whole(exchange(tri_grad.reshape(n, rows * cols // 128, 128)))
    row_own = dot("ij,jk->ik", g, big_r).astype(jnp.bfloat16)
    col_own = dot("ij,ik->jk", g, big_l).astype(jnp.bfloat16)
    back = exchange(jnp.stack([tiled(row_own), tiled(col_own)], axis=1))
    row_part = back[:, 0].reshape(hidden, -1).astype(jnp.float32)
    col_part = back[:, 1].reshape(hidden, -1).astype(jnp.float32)

    def push_back(part, values, sig, weight):
        comb = jnp.concatenate(
            [part * mask * sig, part * mask * values * sig * (1.0 - sig)], axis=0
        ).astype(jnp.bfloat16)
        return (dot("hp,ch->pc", comb, weight), dot("pc,hp->ch", flat, comb))

    from_rows, grad_left = push_back(row_part, left_val, left_sig, left_weight)
    from_cols, grad_right = push_back(col_part, right_val, right_sig, right_weight)
    gate_back = dot("dp,cd->pc", gate_grad, gate_weight)
    normed_grad = (gate_back + from_rows + from_cols).reshape(pair.shape)
    scaled = normed_grad * norm_gain
    grad_pair = (
        pair_scale
        * (
            scaled
            - jnp.mean(scaled, axis=-1, keepdims=True)
            - pair_hat * jnp.mean(scaled * pair_hat, axis=-1, keepdims=True)
        )
    ).astype(jnp.bfloat16)
    grad_norms = jnp.stack(
        [
            jnp.sum(normed_grad * pair_hat, axis=(0, 1)),
            jnp.sum(normed_grad, axis=(0, 1)),
            jnp.sum(tnorm_grad * tri_hat, axis=1),
            jnp.sum(tnorm_grad, axis=1),
        ]
    )
    parts = [grad_left, grad_right, grad_gating, grad_output, grad_norms]
    flat_parts = jnp.concatenate([a.reshape(-1, 128) for a in parts], axis=0)
    size = flat_parts.shape[0]
    per = -(-size // (n * 8)) * 8
    padded = jnp.pad(flat_parts, ((0, per * n - size), (0, 0))).reshape(n, per, 128)
    mine = jnp.sum(exchange(padded), axis=0) * (1.0 / tokens)
    total = lax.all_gather(mine, AXES, axis=0, tiled=True)
    done, at = ([], 0)
    for a in parts:
        count = a.size // 128
        done.append(total[at : at + count].reshape(a.shape))
        at += count
    return (update, grad_pair, *done)


def solution(mesh):
    return jax.shard_map(
        per_device,
        mesh=mesh,
        in_specs=(P("row", "col", None), P("row", "col", None)) + (P(),) * 9,
        out_specs=(P("row", "col", None), P("row", "col", None)) + (P(),) * 5,
        check_vma=False,
    )
```

profile of v0, /device:TPU:0, one launch (start us, length us, event | category | flops | bytes accessed | tf_op | source)
XLA Modules:
  0.0 505.4 jit_solution(2819725478493641133)
XLA Ops:
  1.5 1.4 convert_reduce_fusion
  2.9 1.7 fusion.17
  4.7 1.7 fusion.11
  7.6 0.6 multiply_convert_fusion.7
  8.2 0.7 copy-done.1
  8.9 1.2 copy.32
  10.1 0.4 copy.33
  10.5 1.1 pad_maximum_fusion
  11.7 29.5 %all_to_all.25 = bf16[128,2,16,128]{3,2,1,0:T(8,128)(2,1)S(1)} all-to-all(bf16[128,2,16,128]{3,2,1,0:T(8,128)(2,1)S(1)} %pad_maximum_fusion), channel_id=1, replica_groups=mesh['row'=16,'col'=8] {'row','col'}, dimensions={0} | all-to-all | bytes 2097152 | tf_op jit(solution)/shard_map/all_to_all | solution.py:17
  41.2 1.1 fusion.43
  42.3 1.6 reshape_squeeze.9
  44.0 1.4 copy.35
  45.4 1.9 reshape.175
  47.3 2.6 reshape_squeeze.8
  49.9 2.7 copy.34
  52.6 1.9 reshape.174
  54.5 0.8 copy-done.14
  55.3 1.3 convolution_convert_fusion.2
  56.5 1.6 reshape.176
  58.2 1.2 copy.50
  59.4 1.8 reshape.177
  61.2 18.5 %all_to_all.26 = bf16[128,16,128]{2,1,0:T(8,128)(2,1)S(1)} all-to-all(bf16[128,16,128]{2,1,0:T(8,128)(2,1)S(1)} %reshape.177), channel_id=1, replica_groups=mesh['row'=16,'col'=8] {'row','col'}, dimensions={0} | all-to-all | bytes 1048576 | tf_op jit(solution)/shard_map/all_to_all | solution.py:17
  80.1 0.5 copy-done.5
  80.5 1.5 copy.37
  82.0 0.6 add_convert_fusion
  83.0 1.2 multiply_convert_fusion.5
  84.3 1.1 fusion.29
  85.4 1.7 fusion.24
  87.1 2.4 multiply_convert_fusion.4
  89.4 1.5 copy.38
  90.9 18.2 %all_to_all.27 = bf16[128,16,128]{2,1,0:T(8,128)(2,1)} all-to-all(bf16[128,16,128]{2,1,0:T(8,128)(2,1)S(1)} %copy.38), channel_id=1, replica_groups=mesh['row'=16,'col'=8] {'row','col'}, dimensions={0} | all-to-all | bytes 1048576 | tf_op jit(solution)/shard_map/all_to_all | solution.py:17
  109.1 1.6 reshape.180
  110.8 1.4 copy.39
  112.2 1.9 reshape.181
  114.2 2.3 convolution_convert_fusion
  116.5 1.2 convolution_convert_fusion.1
  117.7 1.6 reshape.182
  119.3 1.2 copy.49
  120.5 2.4 stack_reshape.14
  123.0 1.6 reshape.183
  124.6 1.2 copy.48
  125.8 1.8 stack_reshape.15
  127.6 1.1 pad_maximum_fusion.1
  128.8 1.2 copy.42
  129.9 6.0 %all-to-all-start.3 = ((bf16[128,2,16,128]{3,2,1,0:T(8,128)(2,1)}), bf16[128,2,16,128]{3,2,1,0:T(8,128)(2,1)}, u32[]{:S(2)}, u32[]{:S(2)}) async-start(bf16[128,2,16,128]{3,2,1,0:T(8,128)(2,1)} %copy.42), calls=%async_computation.3 | async-start | bytes 2097152 | tf_op jit(solution)/shard_map/all_to_all | solution.py:17
  136.2 2.2 fusion.48
  138.4 2.2 fusion.47
  140.5 13.3 %all-to-all-done.3 = bf16[128,2,16,128]{3,2,1,0:T(8,128)(2,1)} async-done(((bf16[128,2,16,128]{3,2,1,0:T(8,128)(2,1)}), bf16[128,2,16,128]{3,2,1,0:T(8,128)(2,1)}, u32[]{:S(2)}, u32[]{:S(2)}) %all-to-all-start.3) | async-done | bytes 1048608 | tf_op jit(solution)/shard_map/all_to_all | solution.py:17
  153.8 2.7 slice_convert_fusion.1
  156.5 1.6 copy.43
  158.1 2.6 copy.44
  160.6 2.4 multiply_convert_fusion.3
  164.2 1.4 fusion.36
  165.7 2.3 fusion.42
  168.0 1.0 fusion.16
  169.2 0.8 pad_bitcast_fusion
  170.0 5.3 %all-to-all-start.4 = ((f32[128,8,128]{2,1,0:T(8,128)}), f32[128,8,128]{2,1,0:T(8,128)S(1)}, u32[]{:S(2)}, u32[]{:S(2)}) async-start(f32[128,8,128]{2,1,0:T(8,128)} %pad_bitcast_fusion), calls=%async_computation.4 | async-start | bytes 1048576 | tf_op jit(solution)/shard_map/all_to_all | solution.py:17
  175.4 1.9 fusion.15
  177.3 11.4 %all-to-all-done.4 = f32[128,8,128]{2,1,0:T(8,128)S(1)} async-done(((f32[128,8,128]{2,1,0:T(8,128)}), f32[128,8,128]{2,1,0:T(8,128)S(1)}, u32[]{:S(2)}, u32[]{:S(2)}) %all-to-all-start.4) | async-done | bytes 524320 | tf_op jit(solution)/shard_map/all_to_all | solution.py:17
  188.8 313.9 %all_gather.3 = f32[1024,128]{1,0:T(8,128)S(1)} all-gather(f32[8,128]{1,0:T(8,128)S(1)} %broadcast_multiply_fusion.6), channel_id=1, replica_groups=mesh['row'=16,'col'=8] {'row','col'}, dimensions={0}, use_global_device_ids=true | all-gather | bytes 528384 | tf_op jit(solution)/shard_map/all_gather | solution.py:139
  502.7 0.6 slice.64
  503.3 0.7 fusion.44
  504.0 0.7 reshape.189
  504.7 0.7 reshape.188
  (76 shorter events, 3.9 us)
Async XLA Ops:
  0.6 5.7 %copy-start = (bf16[128,256]{1,0:T(8,128)(2,1)S(1)}, bf16[128,256]{1,0:T(8,128)(2,1)}, u32[]{:S(2)}) copy-start(bf16[128,256]{1,0:T(8,128)(2,1)} %param.17) | copy-start | bytes 196612
  2.9 4.2 copy-start.18
  6.3 0.8 copy-start.6
  7.6 1.3 copy-start.1
  47.3 7.2 %copy-start.9 = (bf16[512,512]{1,0:T(8,128)(2,1)}, bf16[512,512]{1,0:T(8,128)(2,1)S(1)}, u32[]{:S(2)}) copy-start(bf16[512,512]{1,0:T(8,128)(2,1)S(1)} %reshape.175) | copy-start | bytes 1572868
  54.5 0.8 copy-start.14
  61.2 20.8 %copy-start.22 = (f32[128]{0:T(128)S(1)}, f32[128]{0:T(128)}, u32[]{:S(2)}) copy-start(f32[128]{0:T(128)} %param.19) | copy-start | bytes 1540
  61.2 20.8 %copy-start.25 = (f32[128]{0:T(128)S(1)}, f32[128]{0:T(128)}, u32[]{:S(2)}) copy-start(f32[128]{0:T(128)} %param.20) | copy-start | bytes 1540
  79.7 0.8 copy-start.5
  79.7 2.9 copy-start.19
  80.5 2.4 copy-start.20
  82.0 1.0 copy-start.7
  82.6 1.6 copy-start.13
  83.0 1.2 copy-start.15
  85.4 4.1 copy-start.11
  87.0 2.4 copy-start.3
  112.2 4.3 copy-start.10
  128.8 7.1 %copy-start.4 = (f32[2048,128]{1,0:T(8,128)S(1)}, f32[2048,128]{1,0:T(8,128)}, u32[]{:S(2)}) copy-start(f32[2048,128]{1,0:T(8,128)} %copy-done.3) | copy-start | bytes 3145732
  129.9 23.9 %all-to-all-start.3 = ((bf16[128,2,16,128]{3,2,1,0:T(8,128)(2,1)}), bf16[128,2,16,128]{3,2,1,0:T(8,128)(2,1)}, u32[]{:S(2)}, u32[]{:S(2)}) async-start(bf16[128,2,16,128]{3,2,1,0:T(8,128)(2,1)} %copy.42), calls=%async_computation.3 | async-start | bytes 2097152 | tf_op jit(solution)/shard_map/all_to_all | solution.py:17
  160.6 2.4 copy-start.8
  163.9 1.8 copy-start.12
  163.9 1.8 copy-start.21
  165.6 2.4 copy-start.2
  168.0 1.1 copy-start.16
  168.0 1.1 copy-start.17
  168.0 1.1 copy-start.23
  168.0 1.1 copy-start.24
  170.0 18.7 %all-to-all-start.4 = ((f32[128,8,128]{2,1,0:T(8,128)}), f32[128,8,128]{2,1,0:T(8,128)S(1)}, u32[]{:S(2)}, u32[]{:S(2)}) async-start(f32[128,8,128]{2,1,0:T(8,128)} %pad_bitcast_fusion), calls=%async_computation.4 | async-start | bytes 1048576 | tf_op jit(solution)/shard_map/all_to_all | solution.py:17
where the time goes:
time: 507 us; the launch traced here: 505 us
  blocking collectives  380 us (75%)
  local copies, waits for them, and re-layouts  48.8 us (10%)
  waiting for transfers between devices  24.6 us (5%)
  other arithmetic  20.7 us (4%)
  matrix products  18 us (4%)
  starting transfers between devices  11.3 us (2%)
    all_gather x1, blocking collectives, per_device(): total = lax.all_gather(mine, AXES, axis=0, tiled=True)  314 us
    all_to_all x3, blocking collectives, exchange(): return lax.all_to_all(x, AXES, 0, 0, tiled=True)  66.2 us
    all_to_all x2, waiting for transfers between devices, exchange(): return lax.all_to_all(x, AXES, 0, 0, tiled=True)  24.6 us
    dot_general x15, matrix products, dot(): return jnp.einsum(form, a, b, preferred_element_type=jnp.float32)  18 us
    all_to_all x2, starting transfers between devices, exchange(): return lax.all_to_all(x, AXES, 0, 0, tiled=True)  11.3 us
  transfers between devices with their start and end apart: 2, of which 2 were waited for; matrix products, arithmetic and copies ran while one was open for 1% of the time, Pallas kernels for 0%

commit v1 on v0

--- a/solution.py
+++ b/solution.py
@@ -136,7 +136,10 @@
     per = -(-size // (n * 8)) * 8
     padded = jnp.pad(flat_parts, ((0, per * n - size), (0, 0))).reshape(n, per, 128)
     mine = jnp.sum(exchange(padded), axis=0) * (1.0 / tokens)
-    total = lax.all_gather(mine, AXES, axis=0, tiled=True)
+    devices = lax.axis_size(AXES)
+    blocks = jnp.stack([mine for _ in range(devices)])
+    blocks = lax.all_to_all(blocks, AXES, split_axis=0, concat_axis=0)
+    total = jnp.concatenate(blocks, axis=0)
     done, at = ([], 0)
     for a in parts:
         count = a.size // 128

time: 507 us -> 211 us (0.42)
  blocking collectives: 380 us -> 84.7 us
    all_gather x1 -> x0, blocking collectives: 314 us -> none  [per_device(): total = lax.all_gather(mine, AXES, axis=0, tiled=True)]
    all_to_all x3 -> x4, blocking collectives: 66.2 us -> 84.7 us  [exchange(): return lax.all_to_all(x, AXES, 0, 0, tiled=True)]
    all_to_all x0 -> x1, waiting for transfers between devices: none -> 11.4 us  [per_device(): blocks = lax.all_to_all(blocks, AXES, split_axis=0, concat_axis=0)]
    all_to_all x2 -> x1, waiting for transfers between devices: 24.6 us -> 13.3 us  [exchange(): return lax.all_to_all(x, AXES, 0, 0, tiled=True)]
    all_to_all x2 -> x1, starting transfers between devices: 11.3 us -> 5.96 us  [exchange(): return lax.all_to_all(x, AXES, 0, 0, tiled=True)]
  transfers between devices with their start and end apart: 2 -> 2, of which waited for: 2 -> 2; matrix products, arithmetic and copies ran while one was open for 1% -> 3% of each run, Pallas kernels for 0% -> 0%
where the time goes in v1:
time: 211 us; the launch traced here: 210 us
  blocking collectives  84.7 us (40%)
  local copies, waits for them, and re-layouts  48.9 us (23%)
  waiting for transfers between devices  24.6 us (12%)
  other arithmetic  20.7 us (10%)
  matrix products  18 us (9%)
  starting transfers between devices  10.9 us (5%)
    all_to_all x4, blocking collectives, exchange(): return lax.all_to_all(x, AXES, 0, 0, tiled=True)  84.7 us
    dot_general x15, matrix products, dot(): return jnp.einsum(form, a, b, preferred_element_type=jnp.float32)  18 us
    all_to_all x1, waiting for transfers between devices, exchange(): return lax.all_to_all(x, AXES, 0, 0, tiled=True)  13.3 us
    all_to_all x1, waiting for transfers between devices, per_device(): blocks = lax.all_to_all(blocks, AXES, split_axis=0, concat_axis=0)  11.4 us
    reshape x6, local copies, waits for them, and re-layouts, tiled(): t = matrix.reshape(n_row, rows, n_col, cols).transpose(0, 2, 1, 3)  8.55 us
    reshape x4, local copies, waits for them, and re-layouts, whole(): received.reshape(n_row, n_col, rows, cols).transpose(0, 2, 1, 3)  7.37 us
    all_to_all x1, starting transfers between devices, exchange(): return lax.all_to_all(x, AXES, 0, 0, tiled=True)  5.96 us
    transpose x3, local copies, waits for them, and re-layouts, whole(): received.reshape(n_row, n_col, rows, cols).transpose(0, 2, 1, 3)  5.51 us
  transfers between devices with their start and end apart: 2, of which 2 were waited for; matrix products, arithmetic and copies ran while one was open for 3% of the time, Pallas kernels for 0%

profile of v1, /device:TPU:0, one launch (start us, length us, event | category | flops | bytes accessed | tf_op | source)
XLA Modules:
  0.0 209.6 jit_solution(9787341782227586618)
XLA Ops:
  1.5 1.4 convert_reduce_fusion
  2.9 1.7 fusion.17
  4.7 1.7 fusion.11
  7.6 0.6 multiply_convert_fusion.7
  8.2 0.7 copy-done.1
  8.9 1.2 copy.32
  10.1 0.4 copy.33
  10.5 1.1 pad_maximum_fusion
  11.7 29.5 %all_to_all.30 = bf16[128,2,16,128]{3,2,1,0:T(8,128)(2,1)S(1)} all-to-all(bf16[128,2,16,128]{3,2,1,0:T(8,128)(2,1)S(1)} %pad_maximum_fusion), channel_id=1, replica_groups=mesh['row'=16,'col'=8] {'row','col'}, dimensions={0} | all-to-all | bytes 2097152 | tf_op jit(solution)/shard_map/all_to_all | solution.py:17
  41.2 1.1 fusion.43
  42.3 1.6 reshape_squeeze.9
  44.0 1.4 copy.35
  45.4 1.9 reshape.186
  47.3 2.6 %reshape_squeeze.8 = bf16[16,8,32,64]{3,2,1,0:T(8,128)(2,1)} reshape(bf16[128,1,16,128]{3,2,1,0:T(8,128)(2,1)} %get-tuple-element.23) | data formatting | bytes 1048576 | tf_op jit(solution)/shard_map/reshape;squeeze | solution.py:50
  49.9 2.7 %copy.34 = bf16[16,32,8,64]{3,2,1,0:T(8,128)(2,1)} copy(bf16[16,32,8,64]{3,1,2,0:T(8,128)(2,1)} %bitcast.153) | data formatting | bytes 1048576 | tf_op jit(solution)/shard_map/transpose | solution.py:50
  52.6 1.9 reshape.185
  54.5 0.8 copy-done.14
  55.3 1.3 convolution_convert_fusion.2
  56.5 1.6 reshape.187
  58.2 1.2 copy.50
  59.4 1.8 reshape.188
  61.2 18.5 %all_to_all.31 = bf16[128,16,128]{2,1,0:T(8,128)(2,1)S(1)} all-to-all(bf16[128,16,128]{2,1,0:T(8,128)(2,1)S(1)} %reshape.188), channel_id=1, replica_groups=mesh['row'=16,'col'=8] {'row','col'}, dimensions={0} | all-to-all | bytes 1048576 | tf_op jit(solution)/shard_map/all_to_all | solution.py:17
  80.1 0.5 copy-done.5
  80.5 1.5 copy.37
  82.0 0.6 add_convert_fusion
  83.0 1.2 multiply_convert_fusion.5
  84.3 1.1 fusion.29
  85.4 1.7 fusion.24
  87.1 2.4 %multiply_convert_fusion.4 = bf16[128,2048]{0,1:T(8,128)(2,1)} fusion(f32[2048,128]{1,0:T(8,128)S(1)} %get-tuple-element.36, f32[128,16,128]{0,2,1:T(8,128)S(1)} %copy.37, f32[2048]{0:T(1024)S(1)} %get-tuple-element.38, f32[2048]{0:T(1024)S(1)} %get-tuple-element.39, f32[128]{0:T(128)S(1)} %copy-done.22, f32[2048]{0:T(1024)S(1)} %rsqrt_bitcast_fusion, ...), kind=kLoop, calls=%fused_computation.62 | loop fusion | flops 2097152 | bytes 2654720 | tf_op jit(solution)/shard_map/convert_element_type | solution.py:98
  89.4 1.5 copy.38
  90.9 18.2 %all_to_all.32 = bf16[128,16,128]{2,1,0:T(8,128)(2,1)} all-to-all(bf16[128,16,128]{2,1,0:T(8,128)(2,1)S(1)} %copy.38), channel_id=1, replica_groups=mesh['row'=16,'col'=8] {'row','col'}, dimensions={0} | all-to-all | bytes 1048576 | tf_op jit(solution)/shard_map/all_to_all | solution.py:17
  109.1 1.6 reshape.191
  110.8 1.4 copy.39
  112.2 1.9 reshape.192
  114.2 2.3 %convolution_convert_fusion = bf16[512,512]{1,0:T(8,128)(2,1)} fusion(bf16[512,512]{1,0:T(8,128)(2,1)S(1)} %reshape.192, bf16[512,512]{1,0:T(8,128)(2,1)} %copy-done.14), kind=kOutput, calls=%fused_computation.10 | convolution fusion | flops 268697600 | bytes 1572864 | tf_op jit(solution)/shard_map/ij,ik->jk/dot_general | solution.py:62
  116.5 1.2 convolution_convert_fusion.1
  117.7 1.6 reshape.193
  119.3 1.2 copy.49
  120.5 2.4 %stack_reshape.14 = bf16[128,1,16,128]{3,2,0,1:T(8,128)(2,1)} reshape(bf16[16,8,32,64]{3,2,1,0:T(8,128)(2,1)} %bitcast.156) | data formatting | bytes 1048576 | tf_op jit(solution)/shard_map/stack;reshape | solution.py:102
  123.0 1.6 reshape.194
  124.6 1.2 copy.48
  125.8 1.8 stack_reshape.15
  127.6 1.1 pad_maximum_fusion.1
  128.8 1.2 copy.42
  129.9 6.0 %all-to-all-start.3 = ((bf16[128,2,16,128]{3,2,1,0:T(8,128)(2,1)}), bf16[128,2,16,128]{3,2,1,0:T(8,128)(2,1)}, u32[]{:S(2)}, u32[]{:S(2)}) async-start(bf16[128,2,16,128]{3,2,1,0:T(8,128)(2,1)} %copy.42), calls=%async_computation.3 | async-start | bytes 2097152 | tf_op jit(solution)/shard_map/all_to_all | solution.py:17
  136.2 2.2 %fusion.47 = f32[128,128]{1,0:T(8,128)} fusion(bf16[128,2048]{0,1:T(8,128)(2,1)} %copy-done.13, bf16[128,2048]{0,1:T(8,128)(2,1)} %copy-done.11), kind=kOutput, calls=%fused_computation.102 | convolution fusion | flops 67108864 | bytes 1114112 | tf_op jit(solution)/shard_map/hp,cp->hc/dot_general | solution.py:62
  138.4 2.2 %fusion.46 = f32[128,128]{1,0:T(8,128)} fusion(bf16[2048,128]{1,0:T(8,128)(2,1)} %bitcast.148, bf16[128,2048]{0,1:T(8,128)(2,1)} %get-tuple-element.18), kind=kOutput, calls=%fused_computation.101 | convolution fusion | flops 67108864 | bytes 1114112 | tf_op jit(solution)/shard_map/pc,dp->cd/dot_general | solution.py:62
  140.5 13.3 %all-to-all-done.3 = bf16[128,2,16,128]{3,2,1,0:T(8,128)(2,1)} async-done(((bf16[128,2,16,128]{3,2,1,0:T(8,128)(2,1)}), bf16[128,2,16,128]{3,2,1,0:T(8,128)(2,1)}, u32[]{:S(2)}, u32[]{:S(2)}) %all-to-all-start.3) | async-done | bytes 1048608 | tf_op jit(solution)/shard_map/all_to_all | solution.py:17
  153.8 2.7 %slice_convert_fusion.1 = (f32[128,1,16,128]{3,2,1,0:T(8,128)}, f32[128,1,16,128]{3,2,1,0:T(8,128)}) fusion(bf16[128,2,16,128]{3,2,1,0:T(8,128)(2,1)} %all-to-all-done.3), kind=kLoop, calls=%fused_computation.75 | loop fusion | flops 524288 | bytes 3145728 | tf_op jit(solution)/shard_map/convert_element_type | solution.py:103
  156.5 1.6 copy.43
  158.1 2.6 %copy.44 = f32[128,1,16,128]{0,3,2,1:T(8,128)} copy(f32[128,1,16,128]{3,2,1,0:T(8,128)} %get-tuple-element.21) | data formatting | bytes 2097152 | tf_op jit(solution)/shard_map/convert_element_type | solution.py:104
  160.6 2.4 %multiply_convert_fusion.3 = (bf16[128,2048]{0,1:T(8,128)(2,1)S(1)}, bf16[128,2048]{0,1:T(8,128)(2,1)S(1)}, bf16[128,2048]{0,1:T(8,128)(2,1)S(1)}, bf16[128,2048]{0,1:T(8,128)(2,1)S(1)}) fusion(f32[128,1,16,128]{0,3,2,1:T(8,128)S(1)} %copy.43, f32[2048]{0:T(1024)S(1)} %reshape.202, f32[256,2048]{0,1:T(8,128)} %copy-done.1, ...), kind=kLoop, calls=%fused_computation.61 | loop fusion | flops 5767168 | bytes 8396800 | tf_op jit(solution)/shard_map/convert.8
  164.2 1.4 fusion.36
  165.7 2.3 %fusion.42 = (f32[128]{0:T(128)}, f32[2048]{0:T(1024)S(1)}, f32[2048,128]{1,0:T(8,128)S(1)}) fusion(f32[128]{0:T(128)S(1)} %copy-done.21, f32[2048,128]{1,0:T(8,128)S(1)} %fusion.34, f32[2048,128]{1,0:T(8,128)} %fusion.36, bf16[128,2048]{0,1:T(8,128)(2,1)S(1)} %copy-done.12, bf16[128,128]{1,0:T(8,128)(2,1)S(1)} %copy-done.20), kind=kOutput, calls=%fused_computation.97 | convolution fusion | flops 68417408 | bytes 3712000 | tf_op jit(solution)/shard_map/dp,cd->pc/dot_general | solution.py:62
  168.0 1.0 fusion.16
  169.2 18.5 %all_to_all.33 = f32[128,8,128]{2,1,0:T(8,128)S(1)} all-to-all(f32[128,8,128]{2,1,0:T(8,128)S(1)} %pad_bitcast_fusion), channel_id=1, replica_groups=mesh['row'=16,'col'=8] {'row','col'}, dimensions={0} | all-to-all | bytes 1048576 | tf_op jit(solution)/shard_map/all_to_all | solution.py:17
  187.9 0.8 stack.20
  188.7 4.9 %all-to-all-start.5 = ((f32[128,8,128]{2,1,0:T(8,128)}), f32[128,8,128]{2,1,0:T(8,128)S(1)}, u32[]{:S(2)}, u32[]{:S(2)}) async-start(f32[128,8,128]{2,1,0:T(8,128)} %stack.20), calls=%async_computation.5 | async-start | bytes 1048576 | tf_op jit(solution)/shard_map/all_to_all | solution.py:141
  193.7 1.9 fusion.15
  195.6 11.4 %all-to-all-done.5 = f32[128,8,128]{2,1,0:T(8,128)S(1)} async-done(((f32[128,8,128]{2,1,0:T(8,128)}), f32[128,8,128]{2,1,0:T(8,128)S(1)}, u32[]{:S(2)}, u32[]{:S(2)}) %all-to-all-start.5) | async-done | bytes 524320 | tf_op jit(solution)/shard_map/all_to_all | solution.py:141
  207.0 0.6 slice.74
  207.6 0.7 reshape.200
  208.3 0.7 reshape.199
  209.0 0.7 slice_bitcast_fusion
  (77 shorter events, 3.9 us)
Async XLA Ops:
  0.6 5.7 %copy-start = (bf16[128,256]{1,0:T(8,128)(2,1)S(1)}, bf16[128,256]{1,0:T(8,128)(2,1)}, u32[]{:S(2)}) copy-start(bf16[128,256]{1,0:T(8,128)(2,1)} %param.17) | copy-start | bytes 196612
  2.9 4.2 %copy-start.18 = (bf16[128,256]{1,0:T(8,128)(2,1)S(1)}, bf16[128,256]{1,0:T(8,128)(2,1)}, u32[]{:S(2)}) copy-start(bf16[128,256]{1,0:T(8,128)(2,1)} %param.16) | copy-start | bytes 196612
  6.3 0.8 copy-start.6
  7.6 1.3 copy-start.1
  47.3 7.2 %copy-start.9 = (bf16[512,512]{1,0:T(8,128)(2,1)}, bf16[512,512]{1,0:T(8,128)(2,1)S(1)}, u32[]{:S(2)}) copy-start(bf16[512,512]{1,0:T(8,128)(2,1)S(1)} %reshape.186) | copy-start | bytes 1572868
  54.5 0.8 copy-start.14
  61.2 20.8 %copy-start.22 = (f32[128]{0:T(128)S(1)}, f32[128]{0:T(128)}, u32[]{:S(2)}) copy-start(f32[128]{0:T(128)} %param.19) | copy-start | bytes 1540
  61.2 20.8 %copy-start.25 = (f32[128]{0:T(128)S(1)}, f32[128]{0:T(128)}, u32[]{:S(2)}) copy-start(f32[128]{0:T(128)} %param.20) | copy-start | bytes 1540
  79.7 0.8 copy-start.5
  79.7 2.9 %copy-start.19 = (bf16[128,128]{1,0:T(8,128)(2,1)S(1)}, bf16[128,128]{1,0:T(8,128)(2,1)}, u32[]{:S(2)}) copy-start(bf16[128,128]{1,0:T(8,128)(2,1)} %param.21) | copy-start | bytes 98308
  80.5 2.4 %copy-start.20 = (bf16[128,128]{1,0:T(8,128)(2,1)S(1)}, bf16[128,128]{1,0:T(8,128)(2,1)}, u32[]{:S(2)}) copy-start(bf16[128,128]{1,0:T(8,128)(2,1)} %param.18) | copy-start | bytes 98308
  82.0 1.0 copy-start.7
  82.6 1.6 copy-start.13
  83.0 1.2 copy-start.15
  85.4 4.1 %copy-start.11 = (bf16[128,2048]{0,1:T(8,128)(2,1)}, bf16[128,2048]{0,1:T(8,128)(2,1)S(1)}, u32[]{:S(2)}) copy-start(bf16[128,2048]{0,1:T(8,128)(2,1)S(1)} %get-tuple-element.19) | copy-start | bytes 1572868
  87.0 2.4 %copy-start.3 = (f32[2048,128]{1,0:T(8,128)}, f32[2048,128]{1,0:T(8,128)S(1)}, u32[]{:S(2)}) copy-start(f32[2048,128]{1,0:T(8,128)S(1)} %get-tuple-element.36) | copy-start | bytes 3145732
  112.2 4.3 %copy-start.10 = (bf16[512,512]{1,0:T(8,128)(2,1)S(1)}, bf16[512,512]{1,0:T(8,128)(2,1)}, u32[]{:S(2)}) copy-start(bf16[512,512]{1,0:T(8,128)(2,1)} %copy-done.9) | copy-start | bytes 1572868
  128.8 7.1 %copy-start.4 = (f32[2048,128]{1,0:T(8,128)S(1)}, f32[2048,128]{1,0:T(8,128)}, u32[]{:S(2)}) copy-start(f32[2048,128]{1,0:T(8,128)} %copy-done.3) | copy-start | bytes 3145732
  129.9 23.9 %all-to-all-start.3 = ((bf16[128,2,16,128]{3,2,1,0:T(8,128)(2,1)}), bf16[128,2,16,128]{3,2,1,0:T(8,128)(2,1)}, u32[]{:S(2)}, u32[]{:S(2)}) async-start(bf16[128,2,16,128]{3,2,1,0:T(8,128)(2,1)} %copy.42), calls=%async_computation.3 | async-start | bytes 2097152 | tf_op jit(solution)/shard_map/all_to_all | solution.py:17
  160.6 2.4 %copy-start.8 = (bf16[32,64,128]{2,1,0:T(8,128)(2,1)S(1)}, bf16[32,64,128]{2,1,0:T(8,128)(2,1)}, u32[]{:S(2)}) copy-start(bf16[32,64,128]{2,1,0:T(8,128)(2,1)} %copy-done.6) | copy-start | bytes 1572868
  163.9 1.8 copy-start.12
  163.9 1.8 copy-start.21
  165.6 2.4 %copy-start.2 = (bf16[32,64,128]{2,1,0:T(8,128)(2,1)S(1)}, bf16[32,64,128]{2,1,0:T(8,128)(2,1)}, u32[]{:S(2)}) copy-start(bf16[32,64,128]{2,1,0:T(8,128)(2,1)} %param.11) | copy-start | bytes 1572868
  168.0 1.1 copy-start.16
  168.0 1.1 copy-start.17
  168.0 1.1 copy-start.23
  168.0 1.1 copy-start.24
  188.7 18.3 %all-to-all-start.5 = ((f32[128,8,128]{2,1,0:T(8,128)}), f32[128,8,128]{2,1,0:T(8,128)S(1)}, u32[]{:S(2)}, u32[]{:S(2)}) async-start(f32[128,8,128]{2,1,0:T(8,128)} %stack.20), calls=%async_computation.5 | async-start | bytes 1048576 | tf_op jit(solution)/shard_map/all_to_all | solution.py:141
